TPU v7x, 32 devices: a whole 2x2x4 slice. The times are simulated.
32 devices in a mesh: freq: 8 (over z, x), sens: 4 (over y, core).
Axes of the slice: x: 2, y: 2, z: 4, core: 2. Of those that a mesh axis runs over, the one named last changes fastest.
Arguments:
- samples: bfloat16 [128, 608, 420], P('freq', 'sens'), may hold values from -6 to 6
- response_tiles: bfloat16 [448, 2, 608, 21], P('freq', None, 'sens'), may hold values from -0.25 to 0.25
- slot_sensor: int32 [608], P('sens'), may hold values from -1 to 599, as said below
- sensor_noise: float32 [600], replicated, may hold values from 0.02 to 5
- advance_offset: int32 [21], replicated, may hold values from 0 to 419
Outputs:
- outlook_values: bfloat16 [128, 21, 420], P('freq')
- noise_spread: float32 [21], replicated
Inputs may be any that keep to these rules, and one draw needn't show every extreme that they name: `slot_sensor`: every sensor number appears in exactly one slot; the other 8 slots hold -1.
All inputs are finite; a program needn't handle non-finite values.
Results may differ from a plain program's by a relative error of at most 0.0055.
Values may be sent and summed in bfloat16 or wider, within the bound.
A program may use at most 64 MiB of HBM per device.

v0:
```python
import math

import jax
import jax.numpy as jnp
from jax import lax
from jax.sharding import PartitionSpec as P

KEPT_HARMONICS = 448


def angles(first_bin, bin_count, period, factor):
    bin_index = first_bin + lax.iota(jnp.int32, bin_count)
    turn_count = bin_index[:, None] * factor[None, :] % period
    return turn_count.astype(jnp.float32) * (2.0 * math.pi / period)


def forward_table(bin_count, step_count, period):
    phase_angle = angles(0, bin_count, period, lax.iota(jnp.int32, step_count))
    return jnp.stack([jnp.cos(phase_angle), -jnp.sin(phase_angle)]).astype(jnp.bfloat16)


def inverse_table(bin_count, step_count, period):
    bin_index = lax.iota(jnp.int32, bin_count)
    weight = jnp.where(bin_index == 0, 1.0, 2.0).astype(jnp.float32) / period
    phase_angle = angles(0, bin_count, period, lax.iota(jnp.int32, step_count))
    return jnp.stack(
        [weight[:, None] * jnp.cos(phase_angle), -weight[:, None] * jnp.sin(phase_angle)]
    )


def contract(spectra, blocks):

    def product(left, right):
        return jnp.einsum("krs,ksq->kqr", left, right, preferred_element_type=jnp.float32)

    real_part = product(spectra[0], blocks[:, 0]) - product(spectra[1], blocks[:, 1])
    imag_part = product(spectra[0], blocks[:, 1]) + product(spectra[1], blocks[:, 0])
    return jnp.stack([real_part, imag_part])


def rotate(summed, first_bin, advance_offset, period):
    twiddle = angles(first_bin, summed.shape[1], period, advance_offset)[:, :, None]
    cosine = jnp.cos(twiddle)
    sine_part = jnp.sin(twiddle)
    real_part = summed[0] * cosine - summed[1] * sine_part
    imag_part = summed[0] * sine_part + summed[1] * cosine
    return jnp.stack([real_part, imag_part])


def on_device(samples, response_tiles, slot_sensor, sensor_noise, advance_offset):
    highest = lax.Precision.HIGHEST
    bins_dev = response_tiles.shape[0]
    first_bin = lax.axis_index("freq") * bins_dev
    period = 2 * KEPT_HARMONICS
    step_count = samples.shape[2]
    live_slot = (slot_sensor >= 0).astype(jnp.bfloat16)
    blocks = response_tiles * live_slot[None, None, :, None]
    sensor_ids = lax.iota(jnp.int32, sensor_noise.shape[0])
    slot_noise = jnp.sum(
        jnp.where(
            slot_sensor[:, None] == sensor_ids[None, :], sensor_noise[None, :], jnp.float32(0.0)
        ),
        axis=1,
    )
    wide = blocks.astype(jnp.float32)
    power = wide[:, 0] * wide[:, 0] + wide[:, 1] * wide[:, 1]
    bin_index = first_bin + lax.iota(jnp.int32, bins_dev)
    bin_weight = jnp.where(bin_index == 0, 1.0, 2.0).astype(jnp.float32) / period
    per_bin = jnp.einsum("ksq,s->kq", power, slot_noise, precision=highest)
    noise_spread = lax.psum(jnp.dot(bin_weight, per_bin, precision=highest), ("freq", "sens"))
    forward = forward_table(KEPT_HARMONICS, step_count, period)
    spectra = jnp.einsum(
        "rst,ckt->ckrs", samples, forward, preferred_element_type=jnp.float32
    ).astype(jnp.bfloat16)
    partial_value = contract(spectra, lax.all_gather(blocks, "freq", axis=0, tiled=True))
    base_bin = 0
    backward = inverse_table(KEPT_HARMONICS, step_count, period)
    summed = lax.psum(partial_value, "sens")
    shifted = rotate(summed, base_bin, advance_offset, period)
    kept_entries_local = jnp.einsum("ckqr,ckt->rqt", shifted, backward, precision=highest)
    outlook_values = kept_entries_local.astype(jnp.bfloat16)
    return (outlook_values, noise_spread)


def solution(mesh):
    placed = (P("freq", "sens", None), P("freq", None, "sens", None), P("sens"), P(), P())
    return jax.shard_map(
        on_device,
        mesh=mesh,
        in_specs=placed,
        out_specs=(P("freq", None, None), P()),
        check_vma=False,
    )
```

profile of v0, /device:TPU:0, one launch (start us, length us, event | category | flops | bytes accessed | tf_op | source)
XLA Modules:
  0.0 256.4 jit_solution(4376142394990606409)
XLA Ops:
  7.2 0.0 copy-start
  7.2 0.0 all-gather.2.cloned.1.call-start
  7.2 0.8 compare_convert_fusion
  8.1 0.0 copy-start.4
  8.1 0.0 copy-start.5
  8.1 3.6 %fusion.59 = (f32[56,2,152,21]{2,3,0,1:T(8,128)}, bf16[56,2,152,21]{2,3,0,1:T(8,128)(2,1)}) fusion(bf16[152]{0:T(256)(128)(2,1)S(1)} %compare_convert_fusion, bf16[56,2,152,21]{2,1,3,0:T(2,128)(2,1)} %param.6), kind=kLoop, calls=%fused_computation.80 | loop fusion | flops 715008 | bytes 2860336 | tf_op jit(solution)/shard_map/convert_element_type | solution.py:65
  11.7 0.0 all-gather.2.cloned.1.call-update
  11.7 0.0 all-reduce.2.cloned.1.call-start
  11.8 0.0 copy-done.4
  11.8 0.0 copy-done.5
  11.8 0.2 select_reduce_fusion
  12.0 1.9 fusion.10
  13.9 1.9 fusion.17
  15.8 0.1 copy.35
  15.9 0.1 convolution_bitcast_fusion
  16.1 45.9 %psum.15 = f32[21]{0:T(128)} all-reduce(f32[21]{0:T(128)S(1)} %convolution_bitcast_fusion), channel_id=1, replica_groups=mesh['freq'=8,'sens'=4] {'freq','sens'}, use_global_device_ids=true, to_apply=%region_2.3 | all-reduce | flops 21 | bytes 168 | tf_op jit(solution)/shard_map/psum | solution.py:70
  62.0 3.8 %negate_convert_fusion = (bf16[1,448,420]{1,2,0:T(8,128)(2,1)S(1)}, bf16[1,448,420]{1,2,0:T(8,128)(2,1)S(1)}) fusion(), kind=kLoop, calls=%fused_computation.36 | loop fusion | flops 2257920 | bytes 752640 | tf_op jit(solution)/shard_map/convert.1
  65.8 0.0 copy-done
  65.8 2.9 %convolution_convert_fusion = bf16[2,448,16,152]{1,3,2,0:T(8,128)(2,1)S(1)} fusion(bf16[16,152,420]{2,1,0:T(8,128)(2,1)S(1)} %copy-done, bf16[1,448,420]{1,2,0:T(8,128)(2,1)S(1)} %get-tuple-element.16, bf16[1,448,420]{1,2,0:T(8,128)(2,1)S(1)} %get-tuple-element.17), kind=kOutput, calls=%fused_computation.8 | convolution fusion | flops 1834104832 | bytes 7153664 | tf_op jit(solution)/shard_map/rst,ckt->ckrs/dot_general | solution.py:72
  68.7 2.6 %slice_bitcast_fusion.7 = (bf16[448,16,152]{0,2,1:T(8,128)(2,1)}, bf16[448,16,152]{0,2,1:T(8,128)(2,1)}) fusion(bf16[2,448,16,152]{1,3,2,0:T(8,128)(2,1)S(1)} %convolution_convert_fusion), kind=kLoop, calls=%fused_computation.10 | loop fusion | bytes 8716288 | tf_op jit(solution)/shard_map/squeeze | solution.py:36
  71.3 7.4 %copy.24 = bf16[448,16,152]{2,1,0:T(8,128)(2,1)} copy(bf16[448,16,152]{0,2,1:T(8,128)(2,1)} %get-tuple-element.8) | data formatting | bytes 4358144 | tf_op jit(solution)/shard_map/squeeze | solution.py:36
  78.8 7.5 %copy.25 = bf16[448,16,152]{2,1,0:T(8,128)(2,1)} copy(bf16[448,16,152]{0,2,1:T(8,128)(2,1)} %get-tuple-element.9) | data formatting | bytes 4358144 | tf_op jit(solution)/shard_map/squeeze | solution.py:36
  86.3 86.1 %all-gather.2.cloned.1.call-done = bf16[448,2,152,21]{2,3,0,1:T(8,128)(2,1)} async-done(((bf16[56,2,152,21]{2,3,0,1:T(8,128)(2,1)}), bf16[448,2,152,21]{2,3,0,1:T(8,128)(2,1)}) %all-gather.2.cloned.1.call-update) | async-done | bytes 5720080 | tf_op jit(solution)/shard_map/all_gather | solution.py:75
  172.4 0.0 copy-start.1
  172.4 5.3 %fusion = f32[448,21,16]{1,2,0:T(8,128)S(1)} fusion(bf16[448,16,152]{2,1,0:T(8,128)(2,1)} %copy.25, bf16[448,2,152,21]{2,3,0,1:T(8,128)(2,1)} %all-gather.2.cloned.1.call-done), kind=kOutput, calls=%fused_computation.2 | convolution fusion | flops 45760512 | bytes 9777152 | tf_op jit(solution)/shard_map/krs,ksq->kqr/dot_general | solution.py:34
  177.8 1.4 copy-done.1
  179.2 5.5 %add_bitcast_fusion = f32[1,448,21,16]{2,3,1,0:T(8,128)} fusion(f32[448,21,16]{1,2,0:T(8,128)S(1)} %fusion, bf16[448,16,152]{2,1,0:T(8,128)(2,1)} %copy.24, bf16[448,2,152,21]{2,3,0,1:T(8,128)(2,1)S(1)} %copy-done.1), kind=kOutput, calls=%fused_computation.6 | convolution fusion | flops 45911040 | bytes 11956224 | tf_op jit(solution)/shard_map/krs,ksq->kqr/dot_general | solution.py:34
  184.7 3.0 %copy.29 = f32[1,448,21,16]{1,3,2,0:T(8,128)S(1)} copy(f32[1,448,21,16]{2,3,1,0:T(8,128)} %add_bitcast_fusion) | data formatting | bytes 1204224 | tf_op jit(solution)/shard_map/stack | solution.py:38
  187.7 0.0 copy-start.2
  187.7 5.3 %fusion.1 = f32[448,21,16]{1,2,0:T(8,128)S(1)} fusion(bf16[448,16,152]{2,1,0:T(8,128)(2,1)} %copy.24, bf16[448,2,152,21]{2,3,0,1:T(8,128)(2,1)} %all-gather.2.cloned.1.call-done), kind=kOutput, calls=%fused_computation.3 | convolution fusion | flops 45760512 | bytes 9777152 | tf_op jit(solution)/shard_map/krs,ksq->kqr/dot_general | solution.py:34
  193.0 0.0 copy-done.2
  193.0 6.1 %subtract_bitcast_fusion = f32[1,448,21,16]{2,3,1,0:T(8,128)} fusion(f32[448,21,16]{1,2,0:T(8,128)S(1)} %fusion.1, bf16[448,16,152]{2,1,0:T(8,128)(2,1)S(1)} %copy-done.2, bf16[448,2,152,21]{2,3,0,1:T(8,128)(2,1)} %all-gather.2.cloned.1.call-done), kind=kOutput, calls=%fused_computation.7 | convolution fusion | flops 45911040 | bytes 8888320 | tf_op jit(solution)/shard_map/krs,ksq->kqr/dot_general | solution.py:34
  199.2 3.7 %copy.28 = f32[1,448,21,16]{1,3,2,0:T(8,128)} copy(f32[1,448,21,16]{2,3,1,0:T(8,128)} %subtract_bitcast_fusion) | data formatting | bytes 1204224 | tf_op jit(solution)/shard_map/stack | solution.py:38
  202.8 0.0 copy-start.6
  202.8 2.4 pad_maximum_fusion
  205.2 0.0 all-reduce.2.cloned.1.call-update
  205.2 0.0 copy-done.6
  205.2 0.3 fusion.39
  205.5 4.5 %fusion.31 = (f32[1,448,420]{1,2,0:T(8,128)S(1)}, f32[1,448,420]{1,2,0:T(8,128)}) fusion(f32[448]{0:T(512)S(1)} %select_multiply_fusion, f32[448]{0:T(512)S(1)} %fusion.42), kind=kLoop, calls=%fused_computation.43 | loop fusion | flops 2069760 | bytes 1508864 | tf_op jit(solution)/shard_map/mul | solution.py:27
  210.0 33.6 %all-reduce.2.cloned.1.call-done = f32[2,448,21,16]{1,3,2,0:T(8,128)} async-done(((f32[2,448,21,16]{1,3,2,0:T(8,128)}), f32[2,448,21,16]{1,3,2,0:T(8,128)}) %all-reduce.2.cloned.1.call-update) | async-done | bytes 1204240 | tf_op jit(solution)/shard_map/psum | solution.py:78
  243.6 0.0 copy-start.3
  243.6 1.6 multiply_subtract_fusion
  245.2 0.1 pad_maximum_fusion.1
  245.3 0.0 copy-done.3
  245.3 3.4 %fusion.19 = bf16[16,21,420]{2,1,0:T(8,128)(2,1)S(1)} fusion(f32[2,448,21,16]{1,3,2,0:T(8,128)S(1)} %pad_maximum_fusion.1, f32[1,448,420]{1,2,0:T(8,128)S(1)} %copy-done.3, f32[1,448,420]{1,2,0:T(8,128)S(1)} %get-tuple-element.18), kind=kOutput, calls=%fused_computation.29 | convolution fusion | flops 1517839616 | bytes 2991744 | tf_op jit(solution)/shard_map/ckqr,ckt->rqt/dot_general | solution.py:80
  248.7 0.8 copy.31
  (2 shorter events, 0.0 us)
Async XLA Ops:
  7.2 58.6 %copy-start = (bf16[16,152,420]{2,1,0:T(8,128)(2,1)S(1)}, bf16[16,152,420]{2,1,0:T(8,128)(2,1)}, u32[]{:S(2)}) copy-start(bf16[16,152,420]{2,1,0:T(8,128)(2,1)} %param.5) | copy-start | bytes 6128644
  7.2 165.2 %all-gather.2.cloned.1.call-start = ((), (), s32[]{:S(2)}) async-start(), calls=%async_computation | async-start | bytes 12386304 | tf_op jit(solution)/shard_map/all_gather | solution.py:75
  8.1 3.7 %copy-start.4 = (f32[600]{0:T(1024)S(1)}, f32[600]{0:T(1024)}, u32[]{:S(2)}) copy-start(f32[600]{0:T(1024)} %param.8) | copy-start | bytes 7204
  8.1 3.7 %copy-start.5 = (s32[152]{0:T(256)S(1)}, s32[152]{0:T(256)}, u32[]{:S(2)}) copy-start(s32[152]{0:T(256)} %param.7) | copy-start | bytes 1828
  11.7 231.8 %all-reduce.2.cloned.1.call-start = ((), (), s32[]{:S(2)}) async-start(), calls=%async_computation.1 | async-start | bytes 2752512 | tf_op jit(solution)/shard_map/psum | solution.py:78
  172.4 6.8 %copy-start.1 = (bf16[448,2,152,21]{2,3,0,1:T(8,128)(2,1)S(1)}, bf16[448,2,152,21]{2,3,0,1:T(8,128)(2,1)}, u32[]{:S(2)}) copy-start(bf16[448,2,152,21]{2,3,0,1:T(8,128)(2,1)} %all-gather.2.cloned.1.call-done) | copy-start | bytes 17160196
  187.7 5.4 %copy-start.2 = (bf16[448,16,152]{2,1,0:T(8,128)(2,1)S(1)}, bf16[448,16,152]{2,1,0:T(8,128)(2,1)}, u32[]{:S(2)}) copy-start(bf16[448,16,152]{2,1,0:T(8,128)(2,1)} %copy.25) | copy-start | bytes 6537220
  202.8 2.4 copy-start.6
  243.6 1.7 copy-start.3
Sparse Core Ops, SparseCore 0:
  11.9 160.5 all-gather.1
  205.3 38.1 all-reduce.1
where the time goes:
time: 257 us; the launch traced here: 256 us
  waiting for transfers between devices  120 us (47%)
  blocking collectives  45.9 us (18%)
  matrix products  30.6 us (12%)
  local copies, waits for them, and re-layouts  26.6 us (10%)
  other arithmetic  19.2 us (7%)
  between operations  14.2 us (6%)
    all_gather x1, waiting for transfers between devices, on_device(): lax.all_gather(blocks, 'freq', axis=0, tiled=True)  86.1 us
    psum x1, blocking collectives, on_device(): lax.psum(jnp.dot(bin_weight, per_bin, precision=highest), ('freq', 'sens'))  45.9 us
    psum x1, waiting for transfers between devices, on_device(): summed = lax.psum(partial_value, 'sens')  33.6 us
    dot_general x4, matrix products, product(): jnp.einsum('krs,ksq->kqr', left, right, preferred_element_type=jnp.float32)  22.3 us
    squeeze x2, local copies, waits for them, and re-layouts, contract(): spectra[0]  10 us
    squeeze x1, local copies, waits for them, and re-layouts, contract(): spectra[1]  7.52 us
    another operation x2, local copies, waits for them, and re-layouts, contract(): return jnp.stack([real_part, imag_part])  6.64 us
  transfers between devices with their start and end apart: 2, of which 2 were waited for; matrix products, arithmetic and copies ran while one was open for 13% of the time, Pallas kernels for 0%

commit v1 on v0

v1 whole, which is shorter than its diff:
```python
import functools
import math

import jax
import jax.numpy as jnp
import numpy as np
from jax import lax
from jax.experimental import pallas as pl
from jax.experimental.pallas import tpu as pltpu
from jax.sharding import PartitionSpec as P

MESH = pl.DeviceIdType.MESH
HALF = 64
LANES = 128


def make_tables(freq_size, bins_dev, step_count, group, chunks):
    bin_count = freq_size * bins_dev
    period = 2 * bin_count
    slot = np.arange(freq_size * chunks * group)
    block, inside = slot // (chunks * group), slot % (chunks * group)
    live = (inside < bins_dev).astype(np.float64)
    bins = np.where(inside < bins_dev, block * bins_dev + inside, 0)
    turns = bins[:, None] * np.arange(step_count)[None, :] % period
    angle = turns * (2.0 * math.pi / period)
    forward = np.stack([np.cos(angle), -np.sin(angle)]) * live[None, :, None]
    weight = np.where(bins == 0, 1.0, 2.0) / period * live
    inverse = np.stack([np.cos(angle), -np.sin(angle)]) * weight[None, :, None]
    inverse = inverse.reshape(2, freq_size * chunks, group, step_count).transpose(0, 2, 1, 3)
    inverse = inverse.reshape(2 * group * freq_size * chunks, step_count)
    return bins, weight, forward, inverse


def kernel(
    dims,
    tiles, samples, forward, slot_noise, noise_weight, cosine, sine, inverse,
    out, spread,
    held, spectra, z_own, z_send, z_recv, gathered, spread_send, spread_recv,
    own_sem, ring_send, ring_recv, z_send_sem, z_recv_sem, s_send_sem, s_recv_sem,
):
    freq_size, sens_size, chunks, group, sites, count = dims
    rows, slots, step_count = samples.shape
    all_chunks = freq_size * chunks
    per_bin = 2 * rows
    lane_tiles = spectra.shape[0]
    me_f = lax.axis_index("freq")
    me_s = lax.axis_index("sens")
    n = freq_size

    def position_of(index):
        odd, pair = lax.rem(index, 2), index // 2
        return pair * (1 - odd) + (n - 1 - pair) * odd

    def index_of(position):
        high = position // (n // 2)
        return 2 * position * (1 - high) + (2 * (n - 1 - position) + 1) * high

    me_p = position_of(me_f)

    def along(step):
        return index_of(lax.rem(me_p + step + 2 * n, n))

    right, left = along(1), along(-1)
    barrier = pltpu.get_barrier_semaphore()
    for neighbour in (left, right):
        pl.semaphore_signal(barrier, inc=1, device_id={"freq": neighbour}, device_id_type=MESH)
    for d in range(1, sens_size):
        peer = lax.rem(me_s + d, sens_size)
        pl.semaphore_signal(barrier, inc=1, device_id={"sens": peer}, device_id_type=MESH)
    pl.semaphore_wait(barrier, 2 + sens_size - 1)

    cuts = [chunks * i // count for i in range(count + 1)]
    half = count // 2
    pieces = [j for i in range(half) for j in (i, half + i) if cuts[j + 1] > cuts[j]]
    sign_of = (1,) * half + (-1,) * half

    def ring_copy(step, j, received):
        d = sign_of[j]
        low, size = cuts[j], cuts[j + 1] - cuts[j]
        origin = along(-d * (step + (1 if received else 0)))
        block = held.at[origin, pl.ds(low, size)]
        source = tiles.at[pl.ds(low, size)] if step == 0 and not received else block
        return pltpu.make_async_remote_copy(
            src_ref=source, dst_ref=block,
            send_sem=ring_send.at[j, step], recv_sem=ring_recv.at[j, step],
            device_id={"freq": right if d == 1 else left}, device_id_type=MESH,
        )

    for j in pieces:
        ring_copy(0, j, False).start()
    own = pltpu.make_async_copy(tiles, held.at[me_f], own_sem)
    own.start()
    own.wait()

    lane = lax.broadcasted_iota(jnp.int32, (rows, LANES), 1)
    which = (lane % HALF) // sites
    sign = jnp.where(lane < HALF, -1.0, 1.0).astype(jnp.float32)
    spread[...] = jnp.zeros_like(spread)

    def transform(r):
        for c in range(2):
            value = lax.dot_general(
                forward[c], samples[r], (((1,), (1,)), ((), ())),
                preferred_element_type=jnp.float32,
            )
            for tile in range(lane_tiles):
                part = value[:, tile * LANES:min(slots, (tile + 1) * LANES)]
                if part.shape[1] < LANES:
                    part = jnp.concatenate(
                        [part, jnp.zeros((part.shape[0], LANES - part.shape[1]), part.dtype)], axis=1
                    )
                spectra[tile, pl.ds(c * rows + r, part.shape[0], stride=per_bin), :] = part

    def contract(origin, j):
        def body(chunk, carry):
            at = origin * chunks + chunk
            weights = held[origin, chunk]
            first = pl.multiple_of(at * (group * per_bin), group * per_bin)
            parts = [spectra[tile, pl.ds(first, group * per_bin), :] for tile in range(lane_tiles)]
            spec = jnp.concatenate(parts, axis=1)[:, :slots].astype(jnp.bfloat16)
            product = jnp.dot(spec, weights, preferred_element_type=jnp.float32)
            picked = [product[c * rows:(c + 1) * rows] for c in range(2)]
            for i in range(1, group):
                for c in range(2):
                    low = i * per_bin + c * rows
                    picked[c] = jnp.where(which == i, product[low:low + rows], picked[c])
            value = picked[0] + sign * pltpu.roll(picked[1], HALF, 1)
            z_own[pl.ds(pl.multiple_of(at * rows, rows), rows), :] = value
            z_send[at] = value.astype(jnp.bfloat16)
            wide = weights.astype(jnp.float32)
            power = wide * wide * slot_noise[...]
            total = power.reshape(slots // 8, 8, LANES).sum(axis=0)
            spread[...] += total * noise_weight[pl.ds(at, 1), :]
            return carry

        lax.fori_loop(cuts[j], cuts[j + 1], body, 0)

    def z_copies(step, j):
        origin = along(-sign_of[j] * step)
        part = pl.ds(origin * chunks + cuts[j], cuts[j + 1] - cuts[j])
        return [
            pltpu.make_async_remote_copy(
                src_ref=z_send.at[part], dst_ref=z_recv.at[d - 1, part],
                send_sem=z_send_sem.at[d - 1, step * count + j],
                recv_sem=z_recv_sem.at[d - 1, step * count + j],
                device_id={"sens": lax.rem(me_s + d, sens_size)}, device_id_type=MESH,
            )
            for d in range(1, sens_size)
        ]

    tasks = [("transform", r) for r in range(rows)] + [("contract", 0, j) for j in pieces]
    waiting = []

    def flush():
        while waiting:
            for copy in z_copies(*waiting.pop(0)):
                copy.start()

    def run(task):
        if task[0] == "transform":
            transform(task[1])
            return
        _, step, j = task
        contract(along(-sign_of[j] * step), j)
        flush()
        waiting.append((step, j))

    def budget(count):
        for _ in range(min(count, len(tasks))):
            run(tasks.pop(0))

    budget(2)
    for step in range(n - 1):
        for j in pieces:
            ring_copy(step, j, True).wait_recv()
            if step < n - 2:
                ring_copy(step + 1, j, False).start()
            tasks.append(("contract", step + 1, j))
            budget(2)
    budget(len(tasks))
    flush()
    spread_send[...] = spread[...]
    spread_copies = [
        pltpu.make_async_remote_copy(
            src_ref=spread_send, dst_ref=spread_recv.at[d - 1],
            send_sem=s_send_sem.at[d - 1], recv_sem=s_recv_sem.at[d - 1],
            device_id={"sens": lax.rem(me_s + d, sens_size)}, device_id_type=MESH,
        )
        for d in range(1, sens_size)
    ]
    for copy in spread_copies:
        copy.start()
    for step in range(n - 1):
        for j in pieces:
            ring_copy(step, j, False).wait_send()
    for step in range(n):
        for j in pieces:
            for copy in z_copies(step, j):
                copy.wait()
    for copy in spread_copies:
        copy.wait()
    total = spread[...]
    for d in range(1, sens_size):
        total += spread_recv[d - 1]
    spread[...] = total

    def combine(at, carry):
        here = pl.ds(pl.multiple_of(at * rows, rows), rows)
        value = z_own[here, :]
        for d in range(1, sens_size):
            value += z_recv[d - 1, at].astype(jnp.float32)
        z_own[here, :] = value * cosine[pl.ds(at, 1), :] + pltpu.roll(value, HALF, 1) * sine[pl.ds(at, 1), :]
        return carry

    lax.fori_loop(0, all_chunks, combine, 0, unroll=4)

    seat = 32
    together = LANES // seat
    place = lax.broadcasted_iota(jnp.int32, (all_chunks, LANES), 1) // seat
    for base in range(0, rows, together):
        mine = [z_own[pl.ds(base + m, all_chunks, stride=rows), :] for m in range(together)]
        for c in range(2):
            for i in range(group):
                start = c * HALF + i * sites
                value = None
                for m in range(together):
                    moved = pltpu.roll(mine[m], (m * seat - start) % LANES, 1)
                    value = moved if value is None else jnp.where(place == m, moved, value)
                low = (c * group + i) * all_chunks
                gathered[low:low + all_chunks, base * seat:(base + together) * seat] = value.astype(jnp.bfloat16)
    result = lax.dot_general(
        gathered[...], inverse[...], (((0,), (0,)), ((), ())), preferred_element_type=jnp.float32
    )
    for r in range(rows):
        out[r] = result[r * seat:r * seat + sites].astype(jnp.bfloat16)


def on_device(freq_size, sens_size, samples, response_tiles, slot_sensor, sensor_noise, advance_offset):
    bins_dev, _, slots, sites = response_tiles.shape
    rows, _, step_count = samples.shape
    group = HALF // sites
    chunks = -(-bins_dev // group)
    all_chunks = freq_size * chunks
    period = 2 * freq_size * bins_dev
    bins, weight, forward, inverse = make_tables(freq_size, bins_dev, step_count, group, chunks)

    def per_lane(table):
        table = table.reshape(all_chunks, group * sites)
        table = jnp.pad(table, ((0, 0), (0, HALF - group * sites)))
        return jnp.concatenate([table, table], axis=1)

    live_slot = slot_sensor >= 0
    sensor_ids = lax.iota(jnp.int32, sensor_noise.shape[0])
    slot_noise = jnp.sum(
        jnp.where(slot_sensor[:, None] == sensor_ids[None, :], sensor_noise[None, :], jnp.float32(0.0)),
        axis=1,
    )
    slot_noise = jnp.broadcast_to(slot_noise[:, None], (slots, LANES))
    tiles = jnp.where(live_slot[None, None, :, None], response_tiles, jnp.bfloat16(0))
    tiles = jnp.pad(tiles, ((0, chunks * group - bins_dev), (0, 0), (0, 0), (0, 0)))
    tiles = tiles.reshape(chunks, group, 2, slots, sites).transpose(0, 3, 2, 1, 4)
    tiles = tiles.reshape(chunks, slots, 2, group * sites)
    tiles = jnp.pad(tiles, ((0, 0), (0, 0), (0, 0), (0, HALF - group * sites))).reshape(chunks, slots, LANES)

    turns = jnp.asarray(bins, jnp.int32)[:, None] * advance_offset[None, :] % period
    twiddle = turns.astype(jnp.float32) * (2.0 * math.pi / period)
    lane_sign = jnp.where(lax.iota(jnp.int32, LANES) < HALF, -1.0, 1.0).astype(jnp.float32)
    cosine = per_lane(jnp.cos(twiddle))
    sine = per_lane(jnp.sin(twiddle)) * lane_sign[None, :]
    noise_weight = per_lane(jnp.asarray(np.repeat(weight[:, None], sites, axis=1), jnp.float32))

    lane_tiles = -(-slots // LANES)
    peers = sens_size - 1
    count = 4 if peers * freq_size * 4 <= 1024 else 2
    vmem = pl.BlockSpec(memory_space=pltpu.VMEM)
    outlook, spread = pl.pallas_call(
        functools.partial(kernel, (freq_size, sens_size, chunks, group, sites, count)),
        out_shape=(
            jax.ShapeDtypeStruct((rows, sites, step_count), jnp.bfloat16),
            jax.ShapeDtypeStruct((8, LANES), jnp.float32),
        ),
        in_specs=[vmem] * 8,
        out_specs=(vmem, vmem),
        scratch_shapes=[
            pltpu.VMEM((freq_size, chunks, slots, LANES), jnp.bfloat16),
            pltpu.VMEM((lane_tiles, all_chunks * group * 2 * rows, LANES), jnp.float32),
            pltpu.VMEM((all_chunks * rows, LANES), jnp.float32),
            pltpu.VMEM((all_chunks, rows, LANES), jnp.bfloat16),
            pltpu.VMEM((peers, all_chunks, rows, LANES), jnp.bfloat16),
            pltpu.VMEM((2 * group * all_chunks, rows * 32), jnp.bfloat16),
            pltpu.VMEM((8, LANES), jnp.float32),
            pltpu.VMEM((peers, 8, LANES), jnp.float32),
            pltpu.SemaphoreType.DMA,
            pltpu.SemaphoreType.DMA((count, freq_size - 1)),
            pltpu.SemaphoreType.DMA((count, freq_size - 1)),
            pltpu.SemaphoreType.DMA((peers, freq_size * count)),
            pltpu.SemaphoreType.DMA((peers, freq_size * count)),
            pltpu.SemaphoreType.DMA((peers,)),
            pltpu.SemaphoreType.DMA((peers,)),
        ],
        compiler_params=pltpu.CompilerParams(
            collective_id=0, has_side_effects=True, vmem_limit_bytes=60 * 1024 * 1024
        ),
    )(
        tiles, samples, jnp.asarray(forward, jnp.bfloat16), slot_noise, noise_weight,
        cosine, sine, jnp.asarray(inverse, jnp.bfloat16),
    )
    by_lane = jnp.sum(spread, axis=0)
    halves = by_lane[:group * sites] + by_lane[HALF:HALF + group * sites]
    noise_spread = jnp.sum(halves.reshape(group, sites), axis=0)
    return (outlook, noise_spread)


def solution(mesh):
    placed = (P("freq", "sens", None), P("freq", None, "sens", None), P("sens"), P(), P())
    return jax.shard_map(
        functools.partial(on_device, mesh.shape["freq"], mesh.shape["sens"]),
        mesh=mesh,
        in_specs=placed,
        out_specs=(P("freq", None, None), P()),
        check_vma=False,
    )
```

time: 257 us -> 101 us (0.39)
  waiting for transfers between devices: 120 us -> 0 us
  Pallas kernels: 0 us -> 79.3 us
  blocking collectives: 45.9 us -> 0 us
  matrix products: 30.6 us -> 0 us
  other arithmetic: 19.2 us -> 5.52 us
  between operations: 14.2 us -> 0.75 us
  local copies, waits for them, and re-layouts: 26.6 us -> 14.8 us
    all_gather x1 -> x0, waiting for transfers between devices: 86.1 us -> none  [on_device(): lax.all_gather(blocks, 'freq', axis=0, tiled=True)]
    pallas_call x0 -> x1, Pallas kernels: none -> 79.3 us  [on_device(): pl.pallas_call(functools.partial(kernel, (freq_size, sens_size, chunks, g...]
    psum x1 -> x0, blocking collectives: 45.9 us -> none  [on_device(): lax.psum(jnp.dot(bin_weight, per_bin, precision=highest), ('freq', 'sens'))]
    psum x1 -> x0, waiting for transfers between devices: 33.6 us -> none  [on_device(): summed = lax.psum(partial_value, 'sens')]
    dot_general x8 -> x0, matrix products: 30.6 us -> none  [the longest x4 22.3 us: product(): jnp.einsum('krs,ksq->kqr', left, right, preferred_element_type=jnp.float32)]
    squeeze x3 -> x0, local copies, waits for them, and re-layouts: 17.5 us -> none  [the longest x2 10 us: contract(): spectra[0]]
    unnamed x15 -> x10, local copies, waits for them, and re-layouts: 2.31 us -> 9.53 us
    another operation x2 -> x0, local copies, waits for them, and re-layouts: 6.64 us -> none  [contract(): return jnp.stack([real_part, imag_part])]
  transfers between devices with their start and end apart: 2 -> 0, of which waited for: 2 -> 0; matrix products, arithmetic and copies ran while one was open for 13% -> 0% of each run, Pallas kernels for 0% -> 0%
where the time goes in v1:
time: 101 us; the launch traced here: 100 us
  Pallas kernels  79.3 us (79%)
  local copies, waits for them, and re-layouts  14.8 us (15%)
  other arithmetic  5.52 us (5%)
    pallas_call x1, Pallas kernels, on_device(): pl.pallas_call(functools.partial(kernel, (freq_size, sens_size, chunks, g...  79.3 us
    unnamed x10, local copies, waits for them, and re-layouts  9.53 us
    select_n x1, other arithmetic, on_device(): jnp.where(live_slot[None, None, :, None], response_tiles, jnp.bfloat16(0))  2.21 us

profile of v1, /device:TPU:0, one launch (start us, length us, event | category | flops | bytes accessed | tf_op | source)
XLA Modules:
  0.0 100.3 jit_solution(14785162811081360705)
XLA Ops:
  0.6 0.7 broadcast_compare_fusion
  1.3 2.2 %broadcast_select_fusion = bf16[56,2,152,21]{2,1,3,0:T(2,128)(2,1)S(1)} fusion(bf16[56,2,152,21]{2,1,3,0:T(2,128)(2,1)} %param.10, pred[152]{0:T(512)(128)(4,1)S(1)} %broadcast_compare_fusion), kind=kLoop, calls=%fused_computation | loop fusion | flops 357504 | bytes 1430168 | tf_op jit(solution)/shard_map/jit(_where)/select_n | solution.py:259
  3.5 1.1 %pad.18 = bf16[57,2,152,21]{2,1,3,0:T(2,128)(2,1)S(1)} pad(bf16[56,2,152,21]{2,1,3,0:T(2,128)(2,1)S(1)} %broadcast_select_fusion, bf16[]{:T(256)} %constant.13.clone.1), padding=0_1x0_0x0_0x0_0 | pad | bytes 1442786 | tf_op jit(solution)/shard_map/jit(_pad)/pad | solution.py:260
  4.6 7.7 %copy.19 = bf16[19,152,2,63]{3,2,1,0:T(2,128)(2,1)S(1)} copy(bf16[19,152,2,63]{1,2,3,0:T(2,128)(2,1)S(1)} %bitcast.7) | data formatting | bytes 1455552
  12.3 1.5 %pad.19.clone = bf16[19,152,2,64]{3,2,1,0:T(2,128)(2,1)S(1)} pad(bf16[19,152,2,63]{3,2,1,0:T(2,128)(2,1)S(1)} %copy.19, bf16[]{:T(256)} %constant.13.clone.1), padding=0_0x0_0x0_0x0_1 | pad | bytes 1467106 | tf_op jit(solution)/shard_map/jit(_pad)/pad | solution.py:263
  13.8 0.0 copy-start.1
  13.9 0.0 copy-start.2
  13.9 0.0 copy-start
  13.9 0.0 copy-start.3
  13.9 1.6 %reshape.42.tiles = bf16[19,152,128]{2,1,0:T(8,128)(2,1)} reshape(bf16[19,152,2,64]{3,2,1,0:T(2,128)(2,1)S(1)} %pad.19.clone) | data formatting | bytes 1478656 | tf_op jit(solution)/shard_map/reshape | solution.py:263
  15.5 0.0 copy-done.1
  15.5 0.0 copy-done.2
  15.5 0.2 select_reduce_fusion
  15.7 0.7 broadcast_in_dim.49.slot_noise
  16.4 0.0 copy-done
  16.5 0.1 copy.17
  16.6 0.0 copy-done.3
  16.6 0.1 mul.43
  16.7 0.3 fusion.2
  17.1 0.8 pad_maximum_fusion
  17.8 79.3 %shard_map.104 = (bf16[16,21,420]{2,1,0:T(8,128)(2,1)}, f32[8,128]{1,0:T(8,128)}) custom-call(bf16[19,152,128]{2,1,0:T(8,128)(2,1)} %reshape.42.tiles, bf16[16,152,420]{2,1,0:T(8,128)(2,1)} %samples.1, bf16[2,456,420]{2,1,0:T(8,128)(2,1)} %constant.38.clone.forward, f32[152,128]{1,0:T(8,128)} %broadcast_in_dim.49.slot_noise, ...), custom_call_target="tpu_custom_call" | custom-call | tf_op jit(solution)/shard_map/pallas_call | solution.py:276
  97.1 1.8 %copy.18 = bf16[16,21,420]{2,0,1:T(8,128)(2,1)} copy(bf16[16,21,420]{2,1,0:T(8,128)(2,1)} %get-tuple-element.10) | data formatting | bytes 564480
  98.9 0.7 reduce_sum.28
  99.6 0.1 slice_add_fusion
  99.7 0.1 add.27
  99.8 0.5 reduce_sum.29
  (6 shorter events, 0.0 us)
Async XLA Ops:
  13.8 1.7 %copy-start.1 = (f32[600]{0:T(1024)S(1)}, f32[600]{0:T(1024)}, u32[]{:S(2)}) copy-start(f32[600]{0:T(1024)} %param.12) | copy-start | bytes 7204
  13.9 1.7 %copy-start.2 = (s32[152]{0:T(256)S(1)}, s32[152]{0:T(256)}, u32[]{:S(2)}) copy-start(s32[152]{0:T(256)} %param.11) | copy-start | bytes 1828
  13.9 2.6 %copy-start = (s32[152,3]{0,1:T(4,128)S(1)}, s32[152,3]{0,1:T(4,128)}, u32[]{:S(2)}) copy-start(s32[152,3]{0,1:T(4,128)} %constant.53) | copy-start | bytes 5476
  13.9 2.7 %copy-start.3 = (s32[21]{0:T(128)S(1)}, s32[21]{0:T(128)}, u32[]{:S(2)}) copy-start(s32[21]{0:T(128)} %param.13) | copy-start | bytes 256

commit v2 on v1

--- a/solution.py
+++ b/solution.py
@@ -33,10 +33,10 @@
 
 def kernel(
     dims,
-    tiles, samples, forward, slot_noise, noise_weight, cosine, sine, inverse,
+    tiles, samples, forward, slot_facts, sorter, noise_weight, cosine, sine, inverse,
     out, spread,
     held, spectra, z_own, z_send, z_recv, gathered, spread_send, spread_recv,
-    own_sem, ring_send, ring_recv, z_send_sem, z_recv_sem, s_send_sem, s_recv_sem,
+    ring_send, ring_recv, z_send_sem, z_recv_sem, s_send_sem, s_recv_sem,
 ):
     freq_size, sens_size, chunks, group, sites, count = dims
     rows, slots, step_count = samples.shape
@@ -67,7 +67,6 @@
     for d in range(1, sens_size):
         peer = lax.rem(me_s + d, sens_size)
         pl.semaphore_signal(barrier, inc=1, device_id={"sens": peer}, device_id_type=MESH)
-    pl.semaphore_wait(barrier, 2 + sens_size - 1)
 
     cuts = [chunks * i // count for i in range(count + 1)]
     half = count // 2
@@ -79,18 +78,30 @@
         low, size = cuts[j], cuts[j + 1] - cuts[j]
         origin = along(-d * (step + (1 if received else 0)))
         block = held.at[origin, pl.ds(low, size)]
-        source = tiles.at[pl.ds(low, size)] if step == 0 and not received else block
         return pltpu.make_async_remote_copy(
-            src_ref=source, dst_ref=block,
+            src_ref=block, dst_ref=block,
             send_sem=ring_send.at[j, step], recv_sem=ring_recv.at[j, step],
             device_id={"freq": right if d == 1 else left}, device_id_type=MESH,
         )
 
-    for j in pieces:
-        ring_copy(0, j, False).start()
-    own = pltpu.make_async_copy(tiles, held.at[me_f], own_sem)
-    own.start()
-    own.wait()
+    width = group * 2 * sites
+
+    def sort_tiles(j):
+        for chunk in range(cuts[j], cuts[j + 1]):
+            low = chunk * width
+            size = min(width, tiles.shape[0] - low)
+            turned = lax.dot_general(
+                tiles[low:low + size, :], sorter[:size, :], (((0,), (0,)), ((), ())),
+                preferred_element_type=jnp.float32,
+            )
+            held[me_f, chunk] = jnp.where(slot_facts[1] > 0.5, turned, 0.0).astype(jnp.bfloat16)
+
+    for at, j in enumerate(pieces):
+        sort_tiles(j)
+        if at == 0:
+            pl.semaphore_wait(barrier, 2 + sens_size - 1)
+        else:
+            ring_copy(0, pieces[at - 1], False).start()
 
     lane = lax.broadcasted_iota(jnp.int32, (rows, LANES), 1)
     which = (lane % HALF) // sites
@@ -111,8 +122,9 @@
                     )
                 spectra[tile, pl.ds(c * rows + r, part.shape[0], stride=per_bin), :] = part
 
-    def contract(origin, j):
-        def body(chunk, carry):
+    def contract(step, j):
+        origin = along(-sign_of[j] * step)
+        for chunk in range(cuts[j], cuts[j + 1]):
             at = origin * chunks + chunk
             weights = held[origin, chunk]
             first = pl.multiple_of(at * (group * per_bin), group * per_bin)
@@ -128,12 +140,9 @@
             z_own[pl.ds(pl.multiple_of(at * rows, rows), rows), :] = value
             z_send[at] = value.astype(jnp.bfloat16)
             wide = weights.astype(jnp.float32)
-            power = wide * wide * slot_noise[...]
+            power = wide * wide * slot_facts[0]
             total = power.reshape(slots // 8, 8, LANES).sum(axis=0)
             spread[...] += total * noise_weight[pl.ds(at, 1), :]
-            return carry
-
-        lax.fori_loop(cuts[j], cuts[j + 1], body, 0)
 
     def z_copies(step, j):
         origin = along(-sign_of[j] * step)
@@ -148,37 +157,61 @@
             for d in range(1, sens_size)
         ]
 
-    tasks = [("transform", r) for r in range(rows)] + [("contract", 0, j) for j in pieces]
-    waiting = []
-
-    def flush():
-        while waiting:
-            for copy in z_copies(*waiting.pop(0)):
-                copy.start()
-
-    def run(task):
-        if task[0] == "transform":
-            transform(task[1])
-            return
-        _, step, j = task
-        contract(along(-sign_of[j] * step), j)
-        flush()
-        waiting.append((step, j))
-
-    def budget(count):
-        for _ in range(min(count, len(tasks))):
-            run(tasks.pop(0))
-
-    budget(2)
-    for step in range(n - 1):
-        for j in pieces:
+    def receive(step, j, last):
+        ring_copy(step, j, True).wait_recv()
+        if not last:
+            ring_copy(step + 1, j, False).start()
+
+    def send_z(step, j):
+        for copy in z_copies(step, j):
+            copy.start()
+
+    def transforms(low, high):
+        lax.fori_loop(low, high, lambda r, carry: (transform(r), carry)[1], 0)
+
+    ring_copy(0, pieces[-1], False).start()
+    turns = 2 * len(pieces)
+    done = 0
+    for turn in range(turns):
+        receive(turn // len(pieces), pieces[turn % len(pieces)], False)
+        upto = rows * (turn + 1) // turns
+        transforms(done, upto)
+        done = upto
+
+    def both(step, carry):
+        for at, j in enumerate(pieces):
+            receive(step, j, False)
+
+            def one(arrival, inner):
+                contract(arrival, j)
+                return inner
+
+            lax.fori_loop(2 * (step - 2), 2 * (step - 2) + 2, one, 0)
+            for arrival in (2 * (step - 2), 2 * (step - 2) + 1):
+                if at > 0:
+                    send_z(arrival, pieces[at - 1])
+                if at == len(pieces) - 1:
+                    send_z(arrival, j)
+        return carry
+
+    lax.fori_loop(2, 5, both, 0)
+
+    def single(step, carry):
+        for at, j in enumerate(pieces):
             ring_copy(step, j, True).wait_recv()
-            if step < n - 2:
+
+            @pl.when(step < n - 2)
+            def _():
                 ring_copy(step + 1, j, False).start()
-            tasks.append(("contract", step + 1, j))
-            budget(2)
-    budget(len(tasks))
-    flush()
+
+            contract(step + 1, j)
+            if at > 0:
+                send_z(step + 1, pieces[at - 1])
+            if at == len(pieces) - 1:
+                send_z(step + 1, j)
+        return carry
+
+    lax.fori_loop(5, n - 1, single, 0)
     spread_send[...] = spread[...]
     spread_copies = [
         pltpu.make_async_remote_copy(
@@ -202,7 +235,12 @@
     total = spread[...]
     for d in range(1, sens_size):
         total += spread_recv[d - 1]
-    spread[...] = total
+    total = jnp.broadcast_to(jnp.sum(total, axis=0, keepdims=True), total.shape)
+    total = total + pltpu.roll(total, HALF, 1)
+    folded = total
+    for i in range(1, group):
+        folded += pltpu.roll(total, LANES - i * sites, 1)
+    spread[...] = folded
 
     def combine(at, carry):
         here = pl.ds(pl.multiple_of(at * rows, rows), rows)
@@ -255,12 +293,13 @@
         jnp.where(slot_sensor[:, None] == sensor_ids[None, :], sensor_noise[None, :], jnp.float32(0.0)),
         axis=1,
     )
-    slot_noise = jnp.broadcast_to(slot_noise[:, None], (slots, LANES))
-    tiles = jnp.where(live_slot[None, None, :, None], response_tiles, jnp.bfloat16(0))
-    tiles = jnp.pad(tiles, ((0, chunks * group - bins_dev), (0, 0), (0, 0), (0, 0)))
-    tiles = tiles.reshape(chunks, group, 2, slots, sites).transpose(0, 3, 2, 1, 4)
-    tiles = tiles.reshape(chunks, slots, 2, group * sites)
-    tiles = jnp.pad(tiles, ((0, 0), (0, 0), (0, 0), (0, HALF - group * sites))).reshape(chunks, slots, LANES)
+    slot_facts = jnp.stack([slot_noise, live_slot.astype(jnp.float32)])
+    slot_facts = jnp.broadcast_to(slot_facts[:, :, None], (2, slots, LANES))
+    tiles = response_tiles.transpose(0, 3, 1, 2).reshape(bins_dev * 2 * sites, slots)
+    sorter = np.zeros((group, sites, 2, LANES), np.float32)
+    for i, q, c in np.ndindex(group, sites, 2):
+        sorter[i, q, c, c * HALF + i * sites + q] = 1.0
+    sorter = jnp.asarray(sorter.reshape(group * sites * 2, LANES), jnp.bfloat16)
 
     turns = jnp.asarray(bins, jnp.int32)[:, None] * advance_offset[None, :] % period
     twiddle = turns.astype(jnp.float32) * (2.0 * math.pi / period)
@@ -279,7 +318,7 @@
             jax.ShapeDtypeStruct((rows, sites, step_count), jnp.bfloat16),
             jax.ShapeDtypeStruct((8, LANES), jnp.float32),
         ),
-        in_specs=[vmem] * 8,
+        in_specs=[vmem] * 9,
         out_specs=(vmem, vmem),
         scratch_shapes=[
             pltpu.VMEM((freq_size, chunks, slots, LANES), jnp.bfloat16),
@@ -290,7 +329,6 @@
             pltpu.VMEM((2 * group * all_chunks, rows * 32), jnp.bfloat16),
             pltpu.VMEM((8, LANES), jnp.float32),
             pltpu.VMEM((peers, 8, LANES), jnp.float32),
-            pltpu.SemaphoreType.DMA,
             pltpu.SemaphoreType.DMA((count, freq_size - 1)),
             pltpu.SemaphoreType.DMA((count, freq_size - 1)),
             pltpu.SemaphoreType.DMA((peers, freq_size * count)),
@@ -302,12 +340,10 @@
             collective_id=0, has_side_effects=True, vmem_limit_bytes=60 * 1024 * 1024
         ),
     )(
-        tiles, samples, jnp.asarray(forward, jnp.bfloat16), slot_noise, noise_weight,
+        tiles, samples, jnp.asarray(forward, jnp.bfloat16), slot_facts, sorter, noise_weight,
         cosine, sine, jnp.asarray(inverse, jnp.bfloat16),
     )
-    by_lane = jnp.sum(spread, axis=0)
-    halves = by_lane[:group * sites] + by_lane[HALF:HALF + group * sites]
-    noise_spread = jnp.sum(halves.reshape(group, sites), axis=0)
+    noise_spread = spread[0, :sites]
     return (outlook, noise_spread)
 
 

time: 101 us -> 90.2 us (0.89)
  local copies, waits for them, and re-layouts: 14.8 us -> 7.34 us
  other arithmetic: 5.52 us -> 2.8 us
    unnamed x10 -> x3, local copies, waits for them, and re-layouts: 9.53 us -> 1.84 us
    pad x2 -> x0, local copies, waits for them, and re-layouts: 2.62 us -> none  [the longest x1 1.53 us: on_device(): jnp.pad(tiles, ((0, 0), (0, 0), (0, 0), (0, HALF - group * sites)))]
    select_n x1 -> x0, other arithmetic: 2.21 us -> none  [on_device(): jnp.where(live_slot[None, None, :, None], response_tiles, jnp.bfloat16(0))]
    mul x5, local copies, waits for them, and re-layouts: 0.21 us -> 1.55 us  [on_device(): jnp.asarray(bins, jnp.int32)[:, None] * advance_offset[None, :] % period]
    reduce_sum x2 -> x0, other arithmetic: 1.23 us -> none  [the longest x1 0.69 us: on_device(): by_lane = jnp.sum(spread, axis=0)]
    squeeze x0 -> x1, local copies, waits for them, and re-layouts: none -> 1.19 us  [on_device(): noise_spread = spread[0, :sites]]
where the time goes in v2:
time: 90.2 us; the launch traced here: 90 us
  Pallas kernels  79.1 us (88%)
  local copies, waits for them, and re-layouts  7.34 us (8%)
  other arithmetic  2.8 us (3%)
    pallas_call x1, Pallas kernels, on_device(): pl.pallas_call(functools.partial(kernel, (freq_size, sens_size, chunks, g...  79.1 us
    reshape x1, local copies, waits for them, and re-layouts, on_device(): response_tiles.transpose(0, 3, 1, 2).reshape(bins_dev * 2 * sites, slots)  1.96 us
    unnamed x3, local copies, waits for them, and re-layouts  1.84 us

profile of v2, /device:TPU:0, one launch (start us, length us, event | category | flops | bytes accessed | tf_op | source)
XLA Modules:
  0.0 90.0 jit_solution(10577956804481136349)
XLA Ops:
  0.6 0.0 copy-start
  0.7 1.0 %select_reduce_fusion = f32[152]{0:T(256)S(1)} fusion(f32[600]{0:T(1024)} %param.13, s32[152]{0:T(256)} %param.12), kind=kLoop, calls=%fused_computation | loop fusion | flops 273448 | bytes 3616 | tf_op jit(solution)/shard_map/reduce_sum | solution.py:292
  1.6 0.7 compare_convert_fusion
  2.3 0.7 mul.42
  3.0 0.1 mul.43
  3.1 0.7 mul.40
  3.8 0.1 copy.15
  3.9 0.3 fusion.2
  4.3 0.8 pad_maximum_fusion
  5.0 0.8 broadcast_in_dim.34.slot_facts
  5.8 0.0 copy-done
  5.8 2.0 %reshape.29.tiles = bf16[2352,152]{1,0:T(8,128)(2,1)} reshape(bf16[56,21,2,152]{3,2,1,0:T(2,128)(2,1)S(1)} %bitcast.7) | data formatting | bytes 1430016 | tf_op jit(solution)/shard_map/reshape | solution.py:298
  7.8 79.1 %shard_map.113 = (bf16[16,21,420]{2,1,0:T(8,128)(2,1)}, f32[8,128]{1,0:T(8,128)}) custom-call(bf16[2352,152]{1,0:T(8,128)(2,1)} %reshape.29.tiles, bf16[16,152,420]{2,1,0:T(8,128)(2,1)} %samples.1, bf16[2,456,420]{2,1,0:T(8,128)(2,1)} %constant.38.clone.forward, f32[2,152,128]{2,1,0:T(8,128)} %broadcast_in_dim.34.slot_facts, ...), custom_call_target="tpu_custom_call" | custom-call | tf_op jit(solution)/shard_map/pallas_call | solution.py:315
  86.9 1.8 %copy.16 = bf16[16,21,420]{2,0,1:T(8,128)(2,1)} copy(bf16[16,21,420]{2,1,0:T(8,128)(2,1)} %get-tuple-element.10) | data formatting | bytes 564480
  88.8 1.2 %slice_bitcast_fusion = f32[21]{0:T(128)} fusion(f32[8,128]{1,0:T(8,128)} %get-tuple-element.5), kind=kLoop, calls=%fused_computation.13 | loop fusion | bytes 168 | tf_op jit(solution)/shard_map/squeeze | solution.py:346
  (5 shorter events, 0.0 us)
Async XLA Ops:
  0.6 5.2 %copy-start = (bf16[56,2,152,21]{2,1,3,0:T(2,128)(2,1)S(1)}, bf16[56,2,152,21]{2,1,3,0:T(2,128)(2,1)}, u32[]{:S(2)}) copy-start(bf16[56,2,152,21]{2,1,3,0:T(2,128)(2,1)} %param.11) | copy-start | bytes 2145028

commit v3 on v2

--- a/solution.py
+++ b/solution.py
@@ -33,13 +33,13 @@
 
 def kernel(
     dims,
-    tiles, samples, forward, slot_facts, sorter, noise_weight, cosine, sine, inverse,
-    out, spread,
+    tiles, samples_in, forward_in, slot_ids, sensor_noise, sorter, noise_weight, bins, offsets, inverse_in,
+    out, spread, samples, forward, inverse, slot_facts, cosine, sine, load_sem,
     held, spectra, z_own, z_send, z_recv, gathered, spread_send, spread_recv,
     ring_send, ring_recv, z_send_sem, z_recv_sem, s_send_sem, s_recv_sem,
 ):
-    freq_size, sens_size, chunks, group, sites, count = dims
-    rows, slots, step_count = samples.shape
+    freq_size, sens_size, chunks, group, sites, count, period_of = dims
+    rows, slots, step_count = samples_in.shape
     all_chunks = freq_size * chunks
     per_bin = 2 * rows
     lane_tiles = spectra.shape[0]
@@ -69,13 +69,15 @@
         pl.semaphore_signal(barrier, inc=1, device_id={"sens": peer}, device_id_type=MESH)
 
     cuts = [chunks * i // count for i in range(count + 1)]
+    cuts = [cut + cut % 2 for cut in cuts[:-1]] + [chunks]
+    edges = [cut * slots for cut in cuts[:-1]] + [held.shape[1]]
     half = count // 2
     pieces = [j for i in range(half) for j in (i, half + i) if cuts[j + 1] > cuts[j]]
     sign_of = (1,) * half + (-1,) * half
 
     def ring_copy(step, j, received):
         d = sign_of[j]
-        low, size = cuts[j], cuts[j + 1] - cuts[j]
+        low, size = edges[j], edges[j + 1] - edges[j]
         origin = along(-d * (step + (1 if received else 0)))
         block = held.at[origin, pl.ds(low, size)]
         return pltpu.make_async_remote_copy(
@@ -84,6 +86,19 @@
             device_id={"freq": right if d == 1 else left}, device_id_type=MESH,
         )
 
+    loads = [
+        pltpu.make_async_copy(source, target, load_sem.at[at])
+        for at, (source, target) in enumerate(
+            ((forward_in, forward), (samples_in, samples), (inverse_in, inverse))
+        )
+    ]
+    for load in loads:
+        load.start()
+    ids = slot_ids[...]
+    same = ids == lax.broadcasted_iota(jnp.int32, (slots, sensor_noise.shape[1]), 1)
+    found = jnp.sum(jnp.where(same, sensor_noise[...], 0.0), axis=1, keepdims=True)
+    slot_facts[0] = jnp.broadcast_to(found, (slots, LANES))
+    slot_facts[1] = jnp.broadcast_to((ids >= 0).astype(jnp.float32), (slots, LANES))
     width = group * 2 * sites
 
     def sort_tiles(j):
@@ -94,7 +109,7 @@
                 tiles[low:low + size, :], sorter[:size, :], (((0,), (0,)), ((), ())),
                 preferred_element_type=jnp.float32,
             )
-            held[me_f, chunk] = jnp.where(slot_facts[1] > 0.5, turned, 0.0).astype(jnp.bfloat16)
+            held[me_f, chunk * slots:(chunk + 1) * slots] = jnp.where(slot_facts[1] > 0.5, turned, 0.0).astype(jnp.bfloat16)
 
     for at, j in enumerate(pieces):
         sort_tiles(j)
@@ -126,7 +141,7 @@
         origin = along(-sign_of[j] * step)
         for chunk in range(cuts[j], cuts[j + 1]):
             at = origin * chunks + chunk
-            weights = held[origin, chunk]
+            weights = held[origin, chunk * slots:(chunk + 1) * slots]
             first = pl.multiple_of(at * (group * per_bin), group * per_bin)
             parts = [spectra[tile, pl.ds(first, group * per_bin), :] for tile in range(lane_tiles)]
             spec = jnp.concatenate(parts, axis=1)[:, :slots].astype(jnp.bfloat16)
@@ -170,6 +185,14 @@
         lax.fori_loop(low, high, lambda r, carry: (transform(r), carry)[1], 0)
 
     ring_copy(0, pieces[-1], False).start()
+    period = float(period_of)
+    ahead = bins[...] * offsets[...]
+    angle = (ahead - period * jnp.floor(ahead / period)) * (2.0 * math.pi / period)
+    side = lax.broadcasted_iota(jnp.int32, angle.shape, 1)
+    cosine[...] = jnp.cos(angle)
+    sine[...] = jnp.sin(angle) * jnp.where(side < HALF, -1.0, 1.0)
+    for load in loads:
+        load.wait()
     turns = 2 * len(pieces)
     done = 0
     for turn in range(turns):
@@ -284,44 +307,42 @@
 
     def per_lane(table):
         table = table.reshape(all_chunks, group * sites)
-        table = jnp.pad(table, ((0, 0), (0, HALF - group * sites)))
-        return jnp.concatenate([table, table], axis=1)
-
-    live_slot = slot_sensor >= 0
-    sensor_ids = lax.iota(jnp.int32, sensor_noise.shape[0])
-    slot_noise = jnp.sum(
-        jnp.where(slot_sensor[:, None] == sensor_ids[None, :], sensor_noise[None, :], jnp.float32(0.0)),
-        axis=1,
-    )
-    slot_facts = jnp.stack([slot_noise, live_slot.astype(jnp.float32)])
-    slot_facts = jnp.broadcast_to(slot_facts[:, :, None], (2, slots, LANES))
+        table = np.pad(table, ((0, 0), (0, HALF - group * sites)))
+        return jnp.asarray(np.concatenate([table, table], axis=1))
+
     tiles = response_tiles.transpose(0, 3, 1, 2).reshape(bins_dev * 2 * sites, slots)
     sorter = np.zeros((group, sites, 2, LANES), np.float32)
     for i, q, c in np.ndindex(group, sites, 2):
         sorter[i, q, c, c * HALF + i * sites + q] = 1.0
     sorter = jnp.asarray(sorter.reshape(group * sites * 2, LANES), jnp.bfloat16)
 
-    turns = jnp.asarray(bins, jnp.int32)[:, None] * advance_offset[None, :] % period
-    twiddle = turns.astype(jnp.float32) * (2.0 * math.pi / period)
-    lane_sign = jnp.where(lax.iota(jnp.int32, LANES) < HALF, -1.0, 1.0).astype(jnp.float32)
-    cosine = per_lane(jnp.cos(twiddle))
-    sine = per_lane(jnp.sin(twiddle)) * lane_sign[None, :]
-    noise_weight = per_lane(jnp.asarray(np.repeat(weight[:, None], sites, axis=1), jnp.float32))
+    offsets = jnp.tile(advance_offset.astype(jnp.float32), group)
+    offsets = jnp.tile(jnp.pad(offsets, (0, HALF - group * sites)), 2)[None, :]
+    lane_bins = per_lane(np.repeat(bins[:, None], sites, axis=1).astype(np.float32))
+    noise_weight = per_lane(np.repeat(weight[:, None], sites, axis=1).astype(np.float32))
 
     lane_tiles = -(-slots // LANES)
     peers = sens_size - 1
     count = 4 if peers * freq_size * 4 <= 1024 else 2
     vmem = pl.BlockSpec(memory_space=pltpu.VMEM)
+    anywhere = pl.BlockSpec(memory_space=pl.ANY)
     outlook, spread = pl.pallas_call(
-        functools.partial(kernel, (freq_size, sens_size, chunks, group, sites, count)),
+        functools.partial(kernel, (freq_size, sens_size, chunks, group, sites, count, period)),
         out_shape=(
             jax.ShapeDtypeStruct((rows, sites, step_count), jnp.bfloat16),
             jax.ShapeDtypeStruct((8, LANES), jnp.float32),
         ),
-        in_specs=[vmem] * 9,
+        in_specs=[vmem, anywhere, anywhere] + [vmem] * 6 + [anywhere],
         out_specs=(vmem, vmem),
         scratch_shapes=[
-            pltpu.VMEM((freq_size, chunks, slots, LANES), jnp.bfloat16),
+            pltpu.VMEM(samples.shape, jnp.bfloat16),
+            pltpu.VMEM(forward.shape, jnp.bfloat16),
+            pltpu.VMEM(inverse.shape, jnp.bfloat16),
+            pltpu.VMEM((2, slots, LANES), jnp.float32),
+            pltpu.VMEM((all_chunks, LANES), jnp.float32),
+            pltpu.VMEM((all_chunks, LANES), jnp.float32),
+            pltpu.SemaphoreType.DMA((3,)),
+            pltpu.VMEM((freq_size, -(-chunks * slots // 16) * 16, LANES), jnp.bfloat16),
             pltpu.VMEM((lane_tiles, all_chunks * group * 2 * rows, LANES), jnp.float32),
             pltpu.VMEM((all_chunks * rows, LANES), jnp.float32),
             pltpu.VMEM((all_chunks, rows, LANES), jnp.bfloat16),
@@ -340,8 +361,8 @@
             collective_id=0, has_side_effects=True, vmem_limit_bytes=60 * 1024 * 1024
         ),
     )(
-        tiles, samples, jnp.asarray(forward, jnp.bfloat16), slot_facts, sorter, noise_weight,
-        cosine, sine, jnp.asarray(inverse, jnp.bfloat16),
+        tiles, samples, jnp.asarray(forward, jnp.bfloat16), slot_sensor[:, None], sensor_noise[None, :],
+        sorter, noise_weight, lane_bins, offsets, jnp.asarray(inverse, jnp.bfloat16),
     )
     noise_spread = spread[0, :sites]
     return (outlook, noise_spread)

time: 90.2 us -> 89.8 us (level)
  local copies, waits for them, and re-layouts: 7.34 us -> 10.3 us
  other arithmetic: 2.8 us -> 0.66 us
  Pallas kernels: 79.1 us -> 77.9 us
    broadcast_in_dim x1 -> x2, local copies, waits for them, and re-layouts: 0.77 us -> 2.69 us  [the longest x1 1.42 us: on_device(): slot_sensor[:, None]]
    reshape x1, local copies, waits for them, and re-layouts: 1.96 us -> 3.84 us  [on_device(): response_tiles.transpose(0, 3, 1, 2).reshape(bins_dev * 2 * sites, slots)]
    mul x5 -> x0, local copies, waits for them, and re-layouts: 1.55 us -> none  [on_device(): jnp.asarray(bins, jnp.int32)[:, None] * advance_offset[None, :] % period]
    pallas_call x1, Pallas kernels: 79.1 us -> 77.9 us  [on_device(): pl.pallas_call(functools.partial(kernel, (freq_size, sens_size, chunks, g...]
    reduce_sum x1 -> x0, other arithmetic: 0.99 us -> none  [on_device(): jnp.sum(jnp.where(slot_sensor[:, None] == sensor_ids[None, :], sensor_noi...]
    unnamed x3 -> x1, local copies, waits for them, and re-layouts: 1.84 us -> 1.84 us
where the time goes in v3:
time: 89.8 us; the launch traced here: 89.5 us
  Pallas kernels  77.9 us (87%)
  local copies, waits for them, and re-layouts  10.3 us (11%)
    pallas_call x1, Pallas kernels, on_device(): pl.pallas_call(functools.partial(kernel, (freq_size, sens_size, chunks, g...  77.9 us
    reshape x1, local copies, waits for them, and re-layouts, on_device(): response_tiles.transpose(0, 3, 1, 2).reshape(bins_dev * 2 * sites, slots)  3.84 us
    unnamed x1, local copies, waits for them, and re-layouts  1.84 us

profile of v3, /device:TPU:0, one launch (start us, length us, event | category | flops | bytes accessed | tf_op | source)
XLA Modules:
  0.0 89.5 jit_solution(11717600767402394292)
XLA Ops:
  0.6 0.7 convert_element_type.5
  1.3 0.1 tile.7
  1.4 0.6 broadcast_in_dim_tile.3.offsets
  2.0 1.3 %broadcast_in_dim.7.sensor_noise = f32[1,600]{1,0:T(1,128)} reshape(f32[600]{0:T(1024)} %param.13) | data formatting | bytes 4800 | tf_op jit(solution)/shard_map/broadcast_in_dim | solution.py:364
  3.3 1.4 %copy.13.slot_ids = s32[152,1]{1,0:T(8,128)} copy(s32[152,1]{0,1:T(1,128)} %bitcast.5) | data formatting | bytes 1216 | tf_op jit(solution)/shard_map/broadcast_in_dim | solution.py:364
  4.7 3.8 %reshape.9.tiles = bf16[2352,152]{1,0:T(8,128)(2,1)} reshape(bf16[56,21,2,152]{3,2,1,0:T(2,128)(2,1)} %bitcast.4) | data formatting | bytes 1430016 | tf_op jit(solution)/shard_map/reshape | solution.py:313
  8.5 77.9 %shard_map.113 = (bf16[16,21,420]{2,1,0:T(8,128)(2,1)}, f32[8,128]{1,0:T(8,128)}) custom-call(bf16[2352,152]{1,0:T(8,128)(2,1)} %reshape.9.tiles, bf16[16,152,420]{2,1,0:T(8,128)(2,1)} %samples_in.1, bf16[2,456,420]{2,1,0:T(8,128)(2,1)} %constant.16.clone.forward_in, s32[152,1]{1,0:T(8,128)} %copy.13.slot_ids, f32[1,600]{1,0:T(1,128)} %broadcast_in_dim.7.sensor_noise, ...), custom_call_target="tpu_custom_call" | custom-call | tf_op jit(solution)/shard_map/pallas_call | solution.py:329
  86.5 1.8 %copy.14 = bf16[16,21,420]{2,0,1:T(8,128)(2,1)} copy(bf16[16,21,420]{2,1,0:T(8,128)(2,1)} %get-tuple-element.8) | data formatting | bytes 564480
  88.3 1.2 %slice_bitcast_fusion = f32[21]{0:T(128)} fusion(f32[8,128]{1,0:T(8,128)} %get-tuple-element.5), kind=kLoop, calls=%fused_computation | loop fusion | bytes 168 | tf_op jit(solution)/shard_map/squeeze | solution.py:367
  (3 shorter events, 0.0 us)
